TPU v7x, 32 devices: a whole 2x2x4 slice. The times are simulated.
32 devices in a mesh: rows: 8 (over z, y), rhs: 4 (over x, core).
Axes of the slice: x: 2, y: 2, z: 4, core: 2. Of those that a mesh axis runs over, the one named last changes fastest.
Arguments:
- upper_unit: float32 [128, 128, 128], P('rows'), may hold values from -1 to 1, as said below
- lower_unit: float32 [128, 128, 128], P('rows'), may hold values from -1 to 1, as said below
- pivot_inv: float32 [128, 128, 128], P('rows'), may hold values from -0.25 to 2.25
- loss_grad_one: float32 [128, 128, 128], P('rows', 'rhs'), may hold values from -6 to 6
- loss_grad_two: float32 [128, 128, 128], P('rows', 'rhs'), may hold values from -0.1875 to 0.1875
- state_one: float32 [128, 128, 128], P('rows', 'rhs'), may hold values from -0.01171875 to 0.01171875
- state_two: float32 [128, 128, 128], P('rows', 'rhs'), may hold values from -1.5 to 1.5
Outputs:
- operator_grad: float32 [128, 3, 128, 128], P('rhs', None, 'rows')
Inputs may be any that keep to these rules, and one draw needn't show every extreme that they name: `upper_unit`: every block has spectral norm below 1. `lower_unit`: every block has spectral norm below 1.
All inputs are finite; a program needn't handle non-finite values.
Results may differ from a plain program's by a relative error of at most 0.0003.
Values sent between devices are 32-bit elements; how exact they have to be, the bound alone decides.
A program may use at most 128 MiB of HBM per device.

v0:
```python
import functools

import jax
import jax.numpy as jnp
from jax import lax
from jax.experimental import pallas as pl
from jax.experimental.pallas import tpu as pltpu
from jax.sharding import PartitionSpec as P

MESH = pl.DeviceIdType.MESH
F32 = jnp.float32
BF16 = jnp.bfloat16


def halves(x):
    high = x.astype(BF16)
    return high, (x - high.astype(F32)).astype(BF16)


def tall(x):
    return jnp.concatenate(halves(x), axis=0)


def wide(x):
    return jnp.concatenate(halves(x), axis=1)


def product(left, right):
    r = jnp.dot(left, right, preferred_element_type=F32)
    m, n = r.shape[0] // 2, r.shape[1] // 2
    return r[:m, :n] + (r[:m, n:] + r[m:, :n])


def kernel(
    n, nq,
    upper, lower, pivot, grad_one, grad_two, state_one, state_two,
    out,
    acat, pcat, scat, vcat, wcat, mine, maps, ends, arrive, gcat, work, solved,
    packed, shares, states, lhs,
    m_send, m_recv, p_send, p_recv, a_send, a_recv, s_send, s_recv, h_send, h_recv, l_sem,
):
    rows, dirs, width = grad_one.shape
    d = lax.axis_index("rows")
    q = lax.axis_index("rhs")
    cut = width // nq
    groups = rows // nq
    own_states = (state_one, state_two)

    def at(i, size):
        return pl.ds(pl.multiple_of(i * size, size), size)

    def target(direction, k):
        return d + 1 + k if direction == 0 else d - 1 - k

    def sends(direction, k):
        return d + 1 + k < n if direction == 0 else d - 1 - k >= 0

    def gets(direction, k):
        return sends(1 - direction, k)

    def map_copy(direction, k):
        return pltpu.make_async_remote_copy(
            src_ref=mine.at[direction], dst_ref=maps.at[direction, k],
            send_sem=m_send.at[direction, k], recv_sem=m_recv.at[direction, k],
            device_id={"rows": target(direction, k)}, device_id_type=MESH)

    def end_copy(sweep, k):
        return pltpu.make_async_remote_copy(
            src_ref=ends.at[sweep], dst_ref=arrive.at[sweep, k],
            send_sem=p_send.at[sweep, k], recv_sem=p_recv.at[sweep, k],
            device_id={"rows": target(sweep % 2, k)}, device_id_type=MESH)

    def share_copy(which, t, src, dst):
        return pltpu.make_async_remote_copy(
            src_ref=packed.at[which, dst], dst_ref=shares.at[:, which, src],
            send_sem=a_send.at[which, t], recv_sem=a_recv.at[which, t],
            device_id={"rhs": dst}, device_id_type=MESH)

    def state_copy(which, t, src, dst):
        return pltpu.make_async_remote_copy(
            src_ref=own_states[which], dst_ref=states.at[pl.ds(1, rows), which, src],
            send_sem=s_send.at[which, t], recv_sem=s_recv.at[which, t],
            device_id={"rhs": dst}, device_id_type=MESH)

    def halo_copy(direction, which, t, src, dst):
        row, slot = (rows - 1, 0) if direction == 0 else (0, rows + 1)
        return pltpu.make_async_remote_copy(
            src_ref=own_states[which].at[row], dst_ref=states.at[slot, which, src],
            send_sem=h_send.at[direction, which, t], recv_sem=h_recv.at[direction, which, t],
            device_id={"rows": target(direction, 0), "rhs": dst}, device_id_type=MESH)

    def ahead(t):
        return lax.rem(q + t, nq)

    def behind(t):
        return lax.rem(q + nq - t, nq)

    for which in range(2):
        for t in range(1, nq):
            state_copy(which, t - 1, q, ahead(t)).start()
    local = [
        pltpu.make_async_copy(
            own_states[which], states.at[pl.ds(1, rows), which, q], l_sem.at[which])
        for which in range(2)
    ]
    for copy in local:
        copy.start()

    ones = (upper, lower)

    def prepare(i, _):
        vcat[i] = wide(pivot[i])
        for side in range(2):
            acat[side, i] = wide(-ones[side][i])
        gcat[:, at(i, width)] = tall(grad_two[i])
        return 0

    lax.fori_loop(0, rows, prepare, 0)

    last = rows - 1
    for side in range(2):
        first, final = (0, last) if side == 0 else (last, 0)
        pcat[side, :, first * 2 * width:(first + 1) * 2 * width] = acat[side, first]
        scat[side, final * width:(final + 1) * width, :] = acat[side, final]

    def stack(high_low):
        return jnp.concatenate([high_low[:, :width], high_low[:, width:]], axis=0)

    def grow(step, _):
        for side in range(2):
            if side == 0:
                i, prev, j, after = step, step - 1, last - step, last - step + 1
            else:
                i, prev, j, after = last - step, last - step + 1, step, step - 1
            before = stack(pcat[side, :, at(prev, 2 * width)])
            pcat[side, :, at(i, 2 * width)] = wide(product(before, acat[side, i]))
            suffix = product(stack(acat[side, j]), scat[side, at(after, width), :])
            scat[side, at(j, width), :] = wide(suffix)
            mine[side] = suffix
        return 0

    lax.fori_loop(1, rows, grow, 0)

    for k in range(n - 2):
        for direction in range(2):
            @pl.when(sends(direction, k))
            def _():
                map_copy(direction, k).start()

    def send_end(sweep):
        ends[sweep] = -product(gcat[...], scat[sweep % 2])
        for k in range(n - 1):
            @pl.when(sends(sweep % 2, k))
            def _():
                end_copy(sweep, k).start()

    def chain(side, source):
        def link(step, carry):
            i = step if side == 0 else last - step
            y = source[i] + carry
            work[i] = y
            return product(tall(y), acat[side, i])

        lax.fori_loop(0, rows, link, jnp.zeros((dirs, width), F32))

    def relay(direction):
        def one(k, _):
            @pl.when(gets(direction, k))
            def _():
                map_copy(direction, k).wait_recv()

            @pl.when(jnp.logical_not(gets(direction, k)))
            def _():
                maps[direction, k] = jnp.zeros((width, width), F32)

            @pl.when(k == 0)
            def _():
                wcat[direction, 0:width, :] = wide(maps[direction, 0])

            @pl.when(k > 0)
            def _():
                wcat[direction, at(k, width), :] = wide(
                    product(tall(maps[direction, k]), wcat[direction, at(lax.max(k - 1, 0), width), :]))
            return 0

        lax.fori_loop(0, n - 2, one, 0)

    def incoming(sweep):
        for k in range(n - 1):
            @pl.when(gets(sweep % 2, k))
            def _():
                end_copy(sweep, k).wait_recv()

            @pl.when(jnp.logical_not(gets(sweep % 2, k)))
            def _():
                arrive[sweep, k] = jnp.zeros((dirs, width), F32)
        total = arrive[sweep, 0]
        if n > 2:
            rest = jnp.concatenate([arrive[sweep, k] for k in range(1, n - 1)], axis=1)
            total = total + product(tall(rest), wcat[sweep % 2])
        return total

    def spread(side, carry):
        r = jnp.dot(tall(carry), pcat[side], preferred_element_type=F32)
        parts = []
        for i in range(rows):
            c = i * 2 * width
            parts.append(r[:dirs, c:c + width]
                         + (r[:dirs, c + width:c + 2 * width] + r[dirs:, c:c + width]))
        return parts

    def solve(first_sweep, source, between):
        send_end(first_sweep)
        between()
        chain(0, source)
        if first_sweep == 0:
            relay(0)
        carry = incoming(first_sweep)
        parts = [carry] + spread(0, carry)[:-1]
        for i in range(rows):
            z = product(tall(work[i] - parts[i]), vcat[i])
            solved[i] = z
            gcat[:, i * width:(i + 1) * width] = tall(z)
        send_end(first_sweep + 1)
        chain(1, solved)
        if first_sweep == 0:
            relay(1)
        carry = incoming(first_sweep + 1)
        parts = spread(1, carry)[1:] + [carry]
        return [work[i] - parts[i] for i in range(rows)]

    def start_halo():
        for direction in range(2):
            @pl.when(sends(direction, 0))
            def _():
                for which in range(2):
                    for t in range(nq):
                        halo_copy(direction, which, t, q, ahead(t)).start()

    lane = lax.broadcasted_iota(jnp.int32, (dirs, width), 1)

    def share(which, adjoint):
        for g in range(groups):
            for dst in range(nq):
                piece = None
                for ii in range(nq):
                    shift = ((ii - dst) * cut) % width
                    x = adjoint[g * nq + ii]
                    x = pltpu.roll(x, shift, 1) if shift else x
                    piece = x if piece is None else jnp.where(lane >= ii * cut, x, piece)
                packed[which, dst, g] = piece
        for t in range(1, nq):
            share_copy(which, t - 1, q, ahead(t)).start()
        copy = pltpu.make_async_copy(
            packed.at[which, q], shares.at[:, which, q], l_sem.at[2 + which])
        copy.start()
        local.append(copy)

    adjoint_two = solve(0, grad_two, start_halo)
    for i in range(rows):
        total = grad_one[i] + adjoint_two[i]
        solved[i] = total
        gcat[:, i * width:(i + 1) * width] = tall(total)
    adjoint_one = solve(2, solved, lambda: share(1, adjoint_two))
    share(0, adjoint_one)

    for which in range(2):
        for t in range(1, nq):
            state_copy(which, t - 1, behind(t), q).wait_recv()
    for direction in range(2):
        @pl.when(gets(direction, 0))
        def _():
            for which in range(2):
                for t in range(nq):
                    halo_copy(direction, which, t, behind(t), q).wait_recv()

        @pl.when(jnp.logical_not(gets(direction, 0)))
        def _():
            slot = 0 if direction == 0 else rows + 1
            states[slot] = jnp.zeros(states.shape[1:], F32)
    for which in (1, 0):
        for t in range(1, nq):
            share_copy(which, t - 1, behind(t), q).wait_recv()
    for copy in local:
        copy.wait()

    depth = 2 * nq * dirs
    for g in range(groups):
        turned = jnp.transpose(shares[g].reshape(depth, width))
        high, low = halves(turned)
        lhs[0, g * width:(g + 1) * width, :] = high
        lhs[1, g * width:(g + 1) * width, :] = low
    for j in range(rows + 2):
        low_row, high_row = max(j - 2, 0), min(j, last)
        a, b = low_row * cut, (high_row + 1) * cut
        left = jnp.concatenate([lhs[0, a:b, :], lhs[1, a:b, :]], axis=0)
        r = product(left, wide(states[j].reshape(depth, width)))
        for i in range(low_row, high_row + 1):
            piece = {j - 1: 0, j: 1, j - 2: 2}[i]
            out[i, piece] = -r[(i - low_row) * cut:(i - low_row + 1) * cut, :]

    for which in range(2):
        for t in range(1, nq):
            state_copy(which, t - 1, q, ahead(t)).wait_send()
            share_copy(which, t - 1, q, ahead(t)).wait_send()
    for direction in range(2):
        @pl.when(sends(direction, 0))
        def _():
            for which in range(2):
                for t in range(nq):
                    halo_copy(direction, which, t, q, ahead(t)).wait_send()

        for k in range(n - 2):
            @pl.when(sends(direction, k))
            def _():
                map_copy(direction, k).wait_send()
    for sweep in range(4):
        for k in range(n - 1):
            @pl.when(sends(sweep % 2, k))
            def _():
                end_copy(sweep, k).wait_send()


def body(n, nq, *args):
    rows, dirs, width = args[3].shape
    cut = width // nq
    groups = rows // nq
    depth = 2 * nq * dirs
    dma = pltpu.SemaphoreType.DMA
    vmem = pl.BlockSpec(memory_space=pltpu.VMEM)
    result = pl.pallas_call(
        functools.partial(kernel, n, nq),
        out_shape=jax.ShapeDtypeStruct((rows, 3, cut, width), F32),
        in_specs=[vmem] * 7,
        out_specs=vmem,
        scratch_shapes=[
            pltpu.VMEM((2, rows, width, 2 * width), BF16),
            pltpu.VMEM((2, width, rows * 2 * width), BF16),
            pltpu.VMEM((2, rows * width, 2 * width), BF16),
            pltpu.VMEM((rows, width, 2 * width), BF16),
            pltpu.VMEM((2, (n - 2) * width, 2 * width), BF16),
            pltpu.VMEM((2, width, width), F32),
            pltpu.VMEM((2, n - 2, width, width), F32),
            pltpu.VMEM((4, dirs, width), F32),
            pltpu.VMEM((4, n - 1, dirs, width), F32),
            pltpu.VMEM((2 * dirs, rows * width), BF16),
            pltpu.VMEM((rows, dirs, width), F32),
            pltpu.VMEM((rows, dirs, width), F32),
            pltpu.VMEM((2, nq, groups, dirs, width), F32),
            pltpu.VMEM((groups, 2, nq, dirs, width), F32),
            pltpu.VMEM((rows + 2, 2, nq, dirs, width), F32),
            pltpu.VMEM((2, rows * cut, depth), BF16),
            dma((2, n - 2)), dma((2, n - 2)),
            dma((4, n - 1)), dma((4, n - 1)),
            dma((2, nq - 1)), dma((2, nq - 1)),
            dma((2, nq - 1)), dma((2, nq - 1)),
            dma((2, 2, nq)), dma((2, 2, nq)),
            dma((4,)),
        ],
        compiler_params=pltpu.CompilerParams(
            has_side_effects=True, vmem_limit_bytes=60 * 1024 * 1024),
    )(*args)
    return jnp.transpose(result, (2, 1, 0, 3))


def solution(mesh):
    factors = P("rows", None, None)
    vectors = P("rows", "rhs", None)
    return jax.shard_map(
        functools.partial(body, mesh.shape["rows"], mesh.shape["rhs"]),
        mesh=mesh,
        in_specs=(factors,) * 3 + (vectors,) * 4,
        out_specs=P("rhs", None, "rows", None),
        check_vma=False,
    )
```

profile of v0, /device:TPU:1, one launch (start us, length us, event | category | flops | bytes accessed | tf_op | source)
XLA Modules:
  0.0 62.0 jit_solution(5113831620543740641)
XLA Ops:
  0.0 59.5 %shard_map.73 = f32[16,3,32,128]{3,2,1,0:T(8,128)} custom-call(f32[16,128,128]{2,1,0:T(8,128)} %upper.1, f32[16,128,128]{2,1,0:T(8,128)} %lower.1, f32[16,128,128]{2,1,0:T(8,128)} %pivot.1, f32[16,32,128]{2,1,0:T(8,128)} %grad_one.1, f32[16,32,128]{2,1,0:T(8,128)} %grad_two.1, f32[16,32,128]{2,1,0:T(8,128)} %state_one.1, f32[16,32,128]{2,1,0:T(8,128)} %state_two.1), custom_call_target="tpu_custom_call" | custom-call | tf_op jit(solution)/shard_map/pallas_call | solution.py:331
  59.5 2.5 %copy.8 = f32[32,3,16,128]{3,2,1,0:T(8,128)} copy(f32[32,3,16,128]{3,0,1,2:T(8,128)} %bitcast.1) | data formatting | bytes 1572864 | tf_op jit(solution)/shard_map/transpose | solution.py:363
where the time goes:
time: 62.2 us; the launch traced here: 62 us
  Pallas kernels  59.5 us (96%)
  local copies, waits for them, and re-layouts  2.47 us (4%)
    pallas_call x1, Pallas kernels, body(): pl.pallas_call(functools.partial(kernel, n, nq), out_shape=jax.ShapeDtype...  59.5 us
    transpose x1, local copies, waits for them, and re-layouts, body(): return jnp.transpose(result, (2, 1, 0, 3))  2.47 us

commit v1 on v0

--- a/solution.py
+++ b/solution.py
@@ -35,9 +35,9 @@
     n, nq,
     upper, lower, pivot, grad_one, grad_two, state_one, state_two,
     out,
-    acat, pcat, scat, vcat, wcat, mine, maps, ends, arrive, gcat, work, solved,
+    acat, tree, pcat, scat, vcat, wcat, mine, maps, ends, arrive, gcat, work, solved,
     packed, shares, states, lhs,
-    m_send, m_recv, p_send, p_recv, a_send, a_recv, s_send, s_recv, h_send, h_recv, l_sem,
+    m_send, m_recv, f_send, f_recv, p_send, p_recv, a_send, a_recv, s_send, s_recv, t_send, t_recv, h_send, h_recv, l_sem,
 ):
     rows, dirs, width = grad_one.shape
     d = lax.axis_index("rows")
@@ -58,11 +58,24 @@
     def gets(direction, k):
         return sends(1 - direction, k)
 
+    half = width // 2
+    parity = lax.rem(q, 2)
+    partner = q + 1 - 2 * parity
+    pairs = nq // 2
+
     def map_copy(direction, k):
-        return pltpu.make_async_remote_copy(
-            src_ref=mine.at[direction], dst_ref=maps.at[direction, k],
+        part = at(parity, half)
+        return pltpu.make_async_remote_copy(
+            src_ref=mine.at[direction, part], dst_ref=maps.at[direction, k, part],
             send_sem=m_send.at[direction, k], recv_sem=m_recv.at[direction, k],
             device_id={"rows": target(direction, k)}, device_id_type=MESH)
+
+    def map_forward(direction, k, owner):
+        part = at(owner, half)
+        return pltpu.make_async_remote_copy(
+            src_ref=maps.at[direction, k, part], dst_ref=maps.at[direction, k, part],
+            send_sem=f_send.at[direction, k], recv_sem=f_recv.at[direction, k],
+            device_id={"rhs": partner}, device_id_type=MESH)
 
     def end_copy(sweep, k):
         return pltpu.make_async_remote_copy(
@@ -82,6 +95,13 @@
             send_sem=s_send.at[which, t], recv_sem=s_recv.at[which, t],
             device_id={"rhs": dst}, device_id_type=MESH)
 
+    def state_forward(which, t, src):
+        block = states.at[pl.ds(1, rows), which, src]
+        return pltpu.make_async_remote_copy(
+            src_ref=own_states[which] if t == 0 else block, dst_ref=block,
+            send_sem=t_send.at[which, t], recv_sem=t_recv.at[which, t],
+            device_id={"rhs": partner}, device_id_type=MESH)
+
     def halo_copy(direction, which, t, src, dst):
         row, slot = (rows - 1, 0) if direction == 0 else (0, rows + 1)
         return pltpu.make_async_remote_copy(
@@ -95,9 +115,13 @@
     def behind(t):
         return lax.rem(q + nq - t, nq)
 
-    for which in range(2):
-        for t in range(1, nq):
-            state_copy(which, t - 1, q, ahead(t)).start()
+    barrier = pltpu.get_barrier_semaphore()
+    met = [{"rows": lax.rem(d + t, n)} for t in range(1, n)]
+    met += [{"rhs": ahead(t)} for t in range(1, nq)]
+    met += [{"rows": lax.rem(d + s, n), "rhs": ahead(t)} for s in (1, n - 1) for t in range(1, nq)]
+    for other in met:
+        pl.semaphore_signal(barrier, inc=1, device_id=other, device_id_type=MESH)
+
     local = [
         pltpu.make_async_copy(
             own_states[which], states.at[pl.ds(1, rows), which, q], l_sem.at[which])
@@ -118,34 +142,64 @@
     lax.fori_loop(0, rows, prepare, 0)
 
     last = rows - 1
-    for side in range(2):
-        first, final = (0, last) if side == 0 else (last, 0)
-        pcat[side, :, first * 2 * width:(first + 1) * 2 * width] = acat[side, first]
-        scat[side, final * width:(final + 1) * width, :] = acat[side, final]
 
     def stack(high_low):
         return jnp.concatenate([high_low[:, :width], high_low[:, width:]], axis=0)
 
-    def grow(step, _):
-        for side in range(2):
-            if side == 0:
-                i, prev, j, after = step, step - 1, last - step, last - step + 1
-            else:
-                i, prev, j, after = last - step, last - step + 1, step, step - 1
-            before = stack(pcat[side, :, at(prev, 2 * width)])
-            pcat[side, :, at(i, 2 * width)] = wide(product(before, acat[side, i]))
-            suffix = product(stack(acat[side, j]), scat[side, at(after, width), :])
-            scat[side, at(j, width), :] = wide(suffix)
-            mine[side] = suffix
-        return 0
-
-    lax.fori_loop(1, rows, grow, 0)
-
+    def row_of(side, m):
+        return m if side == 0 else last - m
+
+    def branch(side, start, size):
+        if size == 1:
+            return acat[side, row_of(side, start)]
+        return tree[side, rows - 2 * rows // size + start // size]
+
+    size = 2
+    while size <= rows:
+        for start in range(0, rows, size):
+            for side in range(2):
+                value = product(
+                    stack(branch(side, start, size // 2)), branch(side, start + size // 2, size // 2))
+                tree[side, rows - 2 * rows // size + start // size] = wide(value)
+                if size == rows:
+                    mine[side] = value
+        size *= 2
+
+    pl.semaphore_wait(barrier, len(met))
     for k in range(n - 2):
         for direction in range(2):
             @pl.when(sends(direction, k))
             def _():
                 map_copy(direction, k).start()
+    for which in range(2):
+        for t in range(1, pairs):
+            state_copy(which, t - 1, q, ahead(2 * t)).start()
+        state_forward(which, 0, q).start()
+
+    def prefix_at(side, count):
+        i = row_of(side, count - 1)
+        return slice(i * 2 * width, (i + 1) * 2 * width)
+
+    def suffix_at(side, count):
+        i = row_of(side, rows - count)
+        return slice(i * width, (i + 1) * width)
+
+    low = rows
+    while low >= 1:
+        for count in range(low, rows + 1, 2 * low):
+            for side in range(2):
+                start = rows - count
+                if count == low:
+                    pcat[side, :, prefix_at(side, count)] = branch(side, 0, low)
+                    scat[side, suffix_at(side, count), :] = branch(side, start, low)
+                else:
+                    before = pcat[side, :, prefix_at(side, count - low)]
+                    pcat[side, :, prefix_at(side, count)] = wide(
+                        product(stack(before), branch(side, count - low, low)))
+                    after = scat[side, suffix_at(side, count - low), :]
+                    scat[side, suffix_at(side, count), :] = wide(
+                        product(stack(branch(side, start, low)), after))
+        low //= 2
 
     def send_end(sweep):
         ends[sweep] = -product(gcat[...], scat[sweep % 2])
@@ -167,7 +221,7 @@
         def one(k, _):
             @pl.when(gets(direction, k))
             def _():
-                map_copy(direction, k).wait_recv()
+                map_forward(direction, k, 1 - parity).wait_recv()
 
             @pl.when(jnp.logical_not(gets(direction, k)))
             def _():
@@ -214,6 +268,12 @@
         between()
         chain(0, source)
         if first_sweep == 0:
+            for direction in range(2):
+                for k in range(n - 2):
+                    @pl.when(gets(direction, k))
+                    def _():
+                        map_copy(direction, k).wait_recv()
+                        map_forward(direction, k, parity).start()
             relay(0)
         carry = incoming(first_sweep)
         parts = [carry] + spread(0, carry)[:-1]
@@ -261,12 +321,19 @@
         total = grad_one[i] + adjoint_two[i]
         solved[i] = total
         gcat[:, i * width:(i + 1) * width] = tall(total)
-    adjoint_one = solve(2, solved, lambda: share(1, adjoint_two))
+    def pass_on():
+        share(1, adjoint_two)
+        for which in range(2):
+            for t in range(1, pairs):
+                state_copy(which, t - 1, behind(2 * t), q).wait_recv()
+                state_forward(which, t, behind(2 * t)).start()
+
+    adjoint_one = solve(2, solved, pass_on)
     share(0, adjoint_one)
 
     for which in range(2):
-        for t in range(1, nq):
-            state_copy(which, t - 1, behind(t), q).wait_recv()
+        for t in range(pairs):
+            state_forward(which, t, lax.rem(partner + nq - 2 * t, nq)).wait_recv()
     for direction in range(2):
         @pl.when(gets(direction, 0))
         def _():
@@ -297,11 +364,15 @@
         r = product(left, wide(states[j].reshape(depth, width)))
         for i in range(low_row, high_row + 1):
             piece = {j - 1: 0, j: 1, j - 2: 2}[i]
-            out[i, piece] = -r[(i - low_row) * cut:(i - low_row + 1) * cut, :]
+            out[pl.ds(piece * rows + i, cut, stride=3 * rows), :] = (
+                -r[(i - low_row) * cut:(i - low_row + 1) * cut, :])
 
     for which in range(2):
+        for t in range(1, pairs):
+            state_copy(which, t - 1, q, ahead(2 * t)).wait_send()
+        for t in range(pairs):
+            state_forward(which, t, behind(2 * t)).wait_send()
         for t in range(1, nq):
-            state_copy(which, t - 1, q, ahead(t)).wait_send()
             share_copy(which, t - 1, q, ahead(t)).wait_send()
     for direction in range(2):
         @pl.when(sends(direction, 0))
@@ -314,6 +385,10 @@
             @pl.when(sends(direction, k))
             def _():
                 map_copy(direction, k).wait_send()
+
+            @pl.when(gets(direction, k))
+            def _():
+                map_forward(direction, k, parity).wait_send()
     for sweep in range(4):
         for k in range(n - 1):
             @pl.when(sends(sweep % 2, k))
@@ -330,11 +405,12 @@
     vmem = pl.BlockSpec(memory_space=pltpu.VMEM)
     result = pl.pallas_call(
         functools.partial(kernel, n, nq),
-        out_shape=jax.ShapeDtypeStruct((rows, 3, cut, width), F32),
+        out_shape=jax.ShapeDtypeStruct((cut * 3 * rows, width), F32),
         in_specs=[vmem] * 7,
         out_specs=vmem,
         scratch_shapes=[
             pltpu.VMEM((2, rows, width, 2 * width), BF16),
+            pltpu.VMEM((2, rows - 1, width, 2 * width), BF16),
             pltpu.VMEM((2, width, rows * 2 * width), BF16),
             pltpu.VMEM((2, rows * width, 2 * width), BF16),
             pltpu.VMEM((rows, width, 2 * width), BF16),
@@ -351,16 +427,18 @@
             pltpu.VMEM((rows + 2, 2, nq, dirs, width), F32),
             pltpu.VMEM((2, rows * cut, depth), BF16),
             dma((2, n - 2)), dma((2, n - 2)),
+            dma((2, n - 2)), dma((2, n - 2)),
             dma((4, n - 1)), dma((4, n - 1)),
             dma((2, nq - 1)), dma((2, nq - 1)),
-            dma((2, nq - 1)), dma((2, nq - 1)),
+            dma((2, max(nq // 2 - 1, 1))), dma((2, max(nq // 2 - 1, 1))),
+            dma((2, nq // 2)), dma((2, nq // 2)),
             dma((2, 2, nq)), dma((2, 2, nq)),
             dma((4,)),
         ],
         compiler_params=pltpu.CompilerParams(
-            has_side_effects=True, vmem_limit_bytes=60 * 1024 * 1024),
+            collective_id=0, has_side_effects=True, vmem_limit_bytes=60 * 1024 * 1024),
     )(*args)
-    return jnp.transpose(result, (2, 1, 0, 3))
+    return result.reshape(cut, 3, rows, width)
 
 
 def solution(mesh):

time: 62.2 us -> 46.6 us (0.75)
  Pallas kernels: 59.5 us -> 44.4 us
    pallas_call x1, Pallas kernels: 59.5 us -> 44.4 us  [body(): pl.pallas_call(functools.partial(kernel, n, nq), out_shape=jax.ShapeDtype...]
    transpose x1 -> x0, local copies, waits for them, and re-layouts: 2.47 us -> none  [body(): return jnp.transpose(result, (2, 1, 0, 3))]
    unnamed x0 -> x1, local copies, waits for them, and re-layouts: none -> 2.06 us
where the time goes in v1:
time: 46.6 us; the launch traced here: 46.5 us
  Pallas kernels  44.4 us (95%)
  local copies, waits for them, and re-layouts  2.06 us (4%)
    pallas_call x1, Pallas kernels, body(): pl.pallas_call(functools.partial(kernel, n, nq), out_shape=jax.ShapeDtype...  44.4 us
    unnamed x1, local copies, waits for them, and re-layouts  2.06 us

profile of v1, /device:TPU:1, one launch (start us, length us, event | category | flops | bytes accessed | tf_op | source)
XLA Modules:
  0.0 46.5 jit_solution(14555652067891379967)
XLA Ops:
  0.0 44.4 %shard_map.73 = f32[1536,128]{1,0:T(8,128)} custom-call(f32[16,128,128]{2,1,0:T(8,128)} %upper.1, f32[16,128,128]{2,1,0:T(8,128)} %lower.1, f32[16,128,128]{2,1,0:T(8,128)} %pivot.1, f32[16,32,128]{2,1,0:T(8,128)} %grad_one.1, f32[16,32,128]{2,1,0:T(8,128)} %grad_two.1, f32[16,32,128]{2,1,0:T(8,128)} %state_one.1, f32[16,32,128]{2,1,0:T(8,128)} %state_two.1), custom_call_target="tpu_custom_call" | custom-call | tf_op jit(solution)/shard_map/pallas_call | solution.py:406
  44.4 2.1 %copy.9 = f32[32,3,16,128]{3,2,1,0:T(8,128)} copy(f32[32,3,16,128]{3,2,1,0:T(8,128)} %bitcast.1) | data formatting | bytes 1572864

commit v2 on v1

--- a/solution.py
+++ b/solution.py
@@ -133,9 +133,12 @@
     ones = (upper, lower)
 
     def prepare(i, _):
-        vcat[i] = wide(pivot[i])
         for side in range(2):
             acat[side, i] = wide(-ones[side][i])
+        return 0
+
+    def prepare_rest(i, _):
+        vcat[i] = wide(pivot[i])
         gcat[:, at(i, width)] = tall(grad_two[i])
         return 0
 
@@ -175,6 +178,8 @@
         for t in range(1, pairs):
             state_copy(which, t - 1, q, ahead(2 * t)).start()
         state_forward(which, 0, q).start()
+
+    lax.fori_loop(0, rows, prepare_rest, 0)
 
     def prefix_at(side, count):
         i = row_of(side, count - 1)
@@ -345,27 +350,29 @@
         def _():
             slot = 0 if direction == 0 else rows + 1
             states[slot] = jnp.zeros(states.shape[1:], F32)
+    for copy in local[:2]:
+        copy.wait()
+
+    depth = nq * dirs
     for which in (1, 0):
         for t in range(1, nq):
             share_copy(which, t - 1, behind(t), q).wait_recv()
-    for copy in local:
-        copy.wait()
-
-    depth = 2 * nq * dirs
-    for g in range(groups):
-        turned = jnp.transpose(shares[g].reshape(depth, width))
-        high, low = halves(turned)
-        lhs[0, g * width:(g + 1) * width, :] = high
-        lhs[1, g * width:(g + 1) * width, :] = low
-    for j in range(rows + 2):
-        low_row, high_row = max(j - 2, 0), min(j, last)
-        a, b = low_row * cut, (high_row + 1) * cut
-        left = jnp.concatenate([lhs[0, a:b, :], lhs[1, a:b, :]], axis=0)
-        r = product(left, wide(states[j].reshape(depth, width)))
-        for i in range(low_row, high_row + 1):
-            piece = {j - 1: 0, j: 1, j - 2: 2}[i]
-            out[pl.ds(piece * rows + i, cut, stride=3 * rows), :] = (
-                -r[(i - low_row) * cut:(i - low_row + 1) * cut, :])
+        local[3 - which].wait()
+        part = slice(which * depth, (which + 1) * depth)
+        for g in range(groups):
+            high, low = halves(jnp.transpose(shares[g, which].reshape(depth, width)))
+            lhs[0, g * width:(g + 1) * width, part] = high
+            lhs[1, g * width:(g + 1) * width, part] = low
+        for j in range(rows + 2):
+            low_row, high_row = max(j - 2, 0), min(j, last)
+            a, b = low_row * cut, (high_row + 1) * cut
+            left = jnp.concatenate([lhs[0, a:b, part], lhs[1, a:b, part]], axis=0)
+            r = product(left, wide(states[j, which].reshape(depth, width)))
+            for i in range(low_row, high_row + 1):
+                piece = {j - 1: 0, j: 1, j - 2: 2}[i]
+                place = pl.ds(piece * rows + i, cut, stride=3 * rows)
+                term = r[(i - low_row) * cut:(i - low_row + 1) * cut, :]
+                out[place, :] = -term if which == 1 else out[place, :] - term
 
     for which in range(2):
         for t in range(1, pairs):

time: 46.6 us -> 46.7 us (level)
  no operation moved by 1% of the time
where the time goes in v2:
time: 46.7 us; the launch traced here: 46.5 us
  Pallas kernels  44.5 us (95%)
  local copies, waits for them, and re-layouts  2.06 us (4%)
    pallas_call x1, Pallas kernels, body(): pl.pallas_call(functools.partial(kernel, n, nq), out_shape=jax.ShapeDtype...  44.5 us
    unnamed x1, local copies, waits for them, and re-layouts  2.06 us

profile of v2, /device:TPU:1, one launch (start us, length us, event | category | flops | bytes accessed | tf_op | source)
XLA Modules:
  0.0 46.5 jit_solution(12153135156121850888)
XLA Ops:
  0.0 44.5 %shard_map.73 = f32[1536,128]{1,0:T(8,128)} custom-call(f32[16,128,128]{2,1,0:T(8,128)} %upper.1, f32[16,128,128]{2,1,0:T(8,128)} %lower.1, f32[16,128,128]{2,1,0:T(8,128)} %pivot.1, f32[16,32,128]{2,1,0:T(8,128)} %grad_one.1, f32[16,32,128]{2,1,0:T(8,128)} %grad_two.1, f32[16,32,128]{2,1,0:T(8,128)} %state_one.1, f32[16,32,128]{2,1,0:T(8,128)} %state_two.1), custom_call_target="tpu_custom_call" | custom-call | tf_op jit(solution)/shard_map/pallas_call | solution.py:413
  44.5 2.1 %copy.9 = f32[32,3,16,128]{3,2,1,0:T(8,128)} copy(f32[32,3,16,128]{3,2,1,0:T(8,128)} %bitcast.1) | data formatting | bytes 1572864
